TPU v7x, 256 devices: a whole 4x4x8 slice. The times are simulated.
256 devices in a mesh: seq: 256 (over z, x, y, core).
Axes of the slice: x: 4, y: 4, z: 8, core: 2. Of those that a mesh axis runs over, the one named last changes fastest.
Arguments:
- queries: bfloat16 [32768, 4096], P('seq'), may hold values from -48 to 48, as said below
- keys: bfloat16 [32768, 512], P('seq'), may hold values from -6 to 6, as said below
- values: bfloat16 [32768, 512], P('seq'), may hold values from -6 to 6
Outputs:
- attended: bfloat16 [32768, 4096], P('seq')
Inputs may be any that keep to these rules, and one draw needn't show every extreme that they name: queries of every block, with 32 heads of 128 entries per token. keys of every block, with 4 heads of 128 entries per token.
All inputs are finite; a program needn't handle non-finite values.
Results may differ from a plain program's by a relative error of at most 0.0049.
Values may be sent and summed in bfloat16 or wider, within the bound.
A program may use at most 64 MiB of HBM per device.

v0:
```python
import math

import jax
import jax.numpy as jnp
from jax import lax
from jax.sharding import Mesh
from jax.sharding import PartitionSpec as P

QUERY_HEADS = 32
KEY_VALUE_HEADS = 4
HEAD_SIZE = 128
BLOCK_TOKENS = 128
HALO = 64
SEQ = ("seq_0", "seq_1", "seq_2", "seq_3")


def nothing_yet(array, identity):
    return jax.tree.map(
        lambda part, zero: jnp.zeros_like(part) + jnp.asarray(zero, part.dtype), array, identity
    )


def carried_in(array, axes, combine, identity):
    before = start = nothing_yet(array, identity)
    subtotal = array
    for axis in reversed(axes):
        size, index = (lax.axis_size(axis), lax.axis_index(axis))
        pieces = jax.tree.map(lambda part: lax.all_gather(part, axis), subtotal)
        inside, subtotal = (start, start)
        for k in range(size):
            passed = k < index
            subtotal = combine(subtotal, jax.tree.map(lambda part: part[k], pieces))
            inside = jax.tree.map(lambda new, old: jnp.where(passed, new, old), subtotal, inside)
        before = combine(inside, before)
    return before


def from_behind(array, axis, by):
    size = lax.axis_size(axis)
    return lax.ppermute(array, axis, [(i, (i + by) % size) for i in range(size)])


def first_seen(former, latter):
    chosen = former[2][0] > 0
    return tuple((jnp.where(chosen, mine, theirs) for mine, theirs in zip(former, latter)))


def shards(queries, keys, values):
    query_groups = QUERY_HEADS // KEY_VALUE_HEADS
    scale = 1.0 / math.sqrt(HEAD_SIZE)
    position = lax.axis_index(SEQ)
    marker = jnp.ones((1,), jnp.bfloat16)
    neutral = (jnp.zeros_like(keys), jnp.zeros_like(values), jnp.zeros((1,), jnp.bfloat16))
    anchor_keys, anchor_values, unused = carried_in(
        (keys, values, marker), SEQ, first_seen, neutral
    )
    tail_k = keys[BLOCK_TOKENS - HALO :]
    tail_v = values[BLOCK_TOKENS - HALO :]
    halo_keys, halo_values = from_behind((tail_k, tail_v), SEQ, 1)
    joined_keys = jnp.concatenate([anchor_keys, halo_keys, keys], axis=0)
    joined_values = jnp.concatenate([anchor_values, halo_values, values], axis=0)
    row_ids = jnp.arange(BLOCK_TOKENS, dtype=jnp.int32)[:, None]
    col_ids = jnp.arange(BLOCK_TOKENS, dtype=jnp.int32)[None, :]
    visible = jnp.concatenate(
        [
            jnp.broadcast_to(position > 0, (BLOCK_TOKENS, BLOCK_TOKENS)),
            jnp.broadcast_to(position > 0, (BLOCK_TOKENS, HALO)),
            col_ids <= row_ids,
        ],
        axis=1,
    )
    outputs = []
    for key_value_head in range(KEY_VALUE_HEADS):
        query_part = queries[
            :,
            key_value_head
            * query_groups
            * HEAD_SIZE : (key_value_head + 1)
            * query_groups
            * HEAD_SIZE,
        ].reshape(BLOCK_TOKENS, query_groups, HEAD_SIZE)
        key_part = joined_keys[:, key_value_head * HEAD_SIZE : (key_value_head + 1) * HEAD_SIZE]
        value_part = joined_values[:, key_value_head * HEAD_SIZE : (key_value_head + 1) * HEAD_SIZE]
        scores = (
            jnp.einsum("tgd,kd->gtk", query_part, key_part, preferred_element_type=jnp.float32)
            * scale
        )
        scores = jnp.where(visible[None], scores, jnp.float32(-1e30))
        highest = jnp.max(scores, axis=-1, keepdims=True)
        expo = jnp.exp(scores - highest)
        weights = (expo / jnp.sum(expo, axis=-1, keepdims=True)).astype(jnp.bfloat16)
        mixed = jnp.einsum("gtk,kd->tgd", weights, value_part, preferred_element_type=jnp.float32)
        outputs.append(mixed.reshape(BLOCK_TOKENS, query_groups * HEAD_SIZE))
    return jnp.concatenate(outputs, axis=1).astype(jnp.bfloat16)


def solution(mesh):
    finer = Mesh(mesh.devices.reshape(8, 4, 4, 2), ("seq_0", "seq_1", "seq_2", "seq_3"))
    placed = (P(SEQ, None), P(SEQ, None), P(SEQ, None))
    return jax.shard_map(
        shards, mesh=finer, in_specs=placed, out_specs=P(SEQ, None), check_vma=False
    )
```

profile of v0, /device:TPU:96, one launch (start us, length us, event | category | flops | bytes accessed | tf_op | source)
XLA Modules:
  0.0 169.7 jit_solution(11836582135211865858)
XLA Ops:
  6.5 1.3 dynamic-slice
  7.8 0.8 dynamic-update-slice
  8.6 2.4 %all-reduce = bf16[2]{0:T(256)(128)(2,1)S(1)} all-reduce(bf16[2]{0:T(256)(128)(2,1)S(1)} %dynamic-update-slice), channel_id=1, replica_groups=mesh['seq_0'=8,'seq_1'=4,'seq_2'=4,'seq_3'=2] {'seq_3'}, use_global_device_ids=true, to_apply=%add | all-reduce | flops 2 | bytes 8
  11.0 0.6 slice_select_fusion.28
  11.6 1.3 dynamic-slice.1
  12.9 1.4 dynamic-update-slice.1
  14.4 10.7 %all-reduce.1 = bf16[4]{0:T(256)(128)(2,1)S(1)} all-reduce(bf16[4]{0:T(256)(128)(2,1)S(1)} %dynamic-update-slice.1), channel_id=2, replica_groups=mesh['seq_0'=8,'seq_1'=4,'seq_2'=4,'seq_3'=2] {'seq_2'}, use_global_device_ids=true, to_apply=%add.1 | all-reduce | flops 4 | bytes 16
  25.1 0.6 fusion.64
  25.7 1.2 slice_select_fusion.32
  26.9 1.3 dynamic-slice.2
  28.2 1.3 dynamic-update-slice.2
  29.5 10.5 %all-reduce.2 = bf16[4]{0:T(256)(128)(2,1)S(1)} all-reduce(bf16[4]{0:T(256)(128)(2,1)S(1)} %dynamic-update-slice.2), channel_id=3, replica_groups=mesh['seq_0'=8,'seq_1'=4,'seq_2'=4,'seq_3'=2] {'seq_1'}, use_global_device_ids=true, to_apply=%add.2 | all-reduce | flops 4 | bytes 16
  39.9 0.7 fusion.65
  40.6 1.3 slice_select_fusion.29
  43.7 2.2 %all-gather.3 = bf16[256,512]{1,0:T(8,128)(2,1)S(1)} all-gather(bf16[128,512]{1,0:T(8,128)(2,1)} %param.5), channel_id=5, replica_groups=mesh['seq_0'=8,'seq_1'=4,'seq_2'=4,'seq_3'=2] {'seq_3'}, dimensions={0}, use_global_device_ids=true | all-gather | bytes 393216 | tf_op jit(solution)/shard_map/all_gather | solution.py:28
  46.0 13.4 %all-gather.5 = bf16[512,512]{1,0:T(8,128)(2,1)S(1)} all-gather(bf16[128,512]{1,0:T(8,128)(2,1)S(1)} %slice_select_fusion.27), channel_id=7, replica_groups=mesh['seq_0'=8,'seq_1'=4,'seq_2'=4,'seq_3'=2] {'seq_2'}, dimensions={0}, use_global_device_ids=true | all-gather | bytes 655360 | tf_op jit(solution)/shard_map/all_gather | solution.py:28
  59.4 0.6 fusion.27
  60.0 12.9 %all_gather.67 = bf16[4,128,512]{2,1,0:T(8,128)(2,1)S(1)} all-gather(bf16[1,128,512]{2,1,0:T(8,128)(2,1)S(1)} %fusion.27), channel_id=1, replica_groups=mesh['seq_0'=8,'seq_1'=4,'seq_2'=4,'seq_3'=2] {'seq_1'}, dimensions={0}, use_global_device_ids=true | all-gather | bytes 655360 | tf_op jit(solution)/shard_map/all_gather | solution.py:28
  74.2 1.4 slice_select_fusion.21
  75.6 2.0 %all-gather.4 = bf16[256,512]{1,0:T(8,128)(2,1)S(1)} all-gather(bf16[128,512]{1,0:T(8,128)(2,1)S(1)} %copy-done), channel_id=6, replica_groups=mesh['seq_0'=8,'seq_1'=4,'seq_2'=4,'seq_3'=2] {'seq_3'}, dimensions={0}, use_global_device_ids=true | all-gather | bytes 393216 | tf_op jit(solution)/shard_map/all_gather | solution.py:28
  77.6 13.4 %all-gather.6 = bf16[512,512]{1,0:T(8,128)(2,1)S(1)} all-gather(bf16[128,512]{1,0:T(8,128)(2,1)S(1)} %slice_select_fusion.13), channel_id=8, replica_groups=mesh['seq_0'=8,'seq_1'=4,'seq_2'=4,'seq_3'=2] {'seq_2'}, dimensions={0}, use_global_device_ids=true | all-gather | bytes 655360 | tf_op jit(solution)/shard_map/all_gather | solution.py:28
  91.0 0.6 fusion.23
  91.7 12.8 %all_gather.72 = bf16[4,128,512]{2,1,0:T(8,128)(2,1)S(1)} all-gather(bf16[1,128,512]{2,1,0:T(8,128)(2,1)S(1)} %fusion.23), channel_id=1, replica_groups=mesh['seq_0'=8,'seq_1'=4,'seq_2'=4,'seq_3'=2] {'seq_1'}, dimensions={0}, use_global_device_ids=true | all-gather | bytes 655360 | tf_op jit(solution)/shard_map/all_gather | solution.py:28
  104.4 1.4 slice_select_fusion.7
  105.8 0.6 slice.240
  106.5 0.6 slice.260
  107.1 0.6 dynamic-slice.3
  107.7 1.4 dynamic-update-slice.3
  109.2 16.1 %all-reduce.3 = bf16[8]{0:T(256)(128)(2,1)S(1)} all-reduce(bf16[8]{0:T(256)(128)(2,1)S(1)} %dynamic-update-slice.3), channel_id=4, replica_groups=mesh['seq_0'=8,'seq_1'=4,'seq_2'=4,'seq_3'=2] {'seq_0'}, use_global_device_ids=true, to_apply=%add.3 | all-reduce | flops 8 | bytes 32
  125.3 0.7 fusion.63
  138.5 2.0 %fusion.62 = (bf16[128,1024]{1,0:T(8,128)(2,1)}, bf16[128,1024]{1,0:T(8,128)(2,1)S(1)}, bf16[128,1024]{1,0:T(8,128)(2,1)S(1)}, bf16[128,1024]{1,0:T(8,128)(2,1)S(1)}) fusion(bf16[128,4096]{1,0:T(8,128)(2,1)} %param.3), kind=kLoop, calls=%fused_computation.119 | loop fusion | bytes 2097152 | tf_op jit(solution)/shard_map/slice | solution.py:74
  140.5 1.8 %copy.36 = bf16[128,1024]{0,1:T(8,128)(2,1)} copy(bf16[128,1024]{1,0:T(8,128)(2,1)} %get-tuple-element.5) | data formatting | bytes 524288
  142.3 0.8 copy.37
  143.1 0.9 copy.38
  144.0 0.8 copy.39
  145.0 2.9 %fusion.26 = bf16[128,512]{1,0:T(8,128)(2,1)S(1)} fusion(bf16[8,128,512]{2,1,0:T(8,128)(2,1)} %all-gather.10.cloned.1.call-done, pred[]{:T(512)} %gt.211, pred[]{:T(512)} %gt.212, pred[]{:T(512)} %bitcast.41, pred[]{:T(512)} %gt.213, pred[]{:T(512)} %gt.216, pred[]{:T(512)} %gt.217, pred[]{:T(512)} %bitcast.12, pred[]{:T(512)} %gt.166, pred[]{:T(512)} %gt.181, ...), kind=kLoop, calls=%fused_computation.57 | loop fusion | flops 2359296 | bytes 2490404 | tf_op jit(solution)/shard_map/jit(_where)/select_n | solution.py:45
  148.0 2.7 %all-gather.12.cloned.1.call-done = bf16[8,128,512]{2,1,0:T(8,128)(2,1)} async-done(((bf16[1,128,512]{2,1,0:T(8,128)(2,1)}), bf16[8,128,512]{2,1,0:T(8,128)(2,1)}) %all-gather.12.cloned.1.call-update) | async-done | bytes 1048592 | tf_op jit(solution)/shard_map/all_gather | solution.py:28
  150.6 2.9 %fusion.22 = bf16[128,512]{1,0:T(8,128)(2,1)S(1)} fusion(bf16[8,128,512]{2,1,0:T(8,128)(2,1)} %all-gather.12.cloned.1.call-done, pred[]{:T(512)} %gt.211, pred[]{:T(512)} %gt.212, pred[]{:T(512)} %bitcast.41, pred[]{:T(512)} %gt.213, pred[]{:T(512)} %gt.216, pred[]{:T(512)} %gt.217, pred[]{:T(512)} %bitcast.12, pred[]{:T(512)} %gt.166, pred[]{:T(512)} %gt.181, ...), kind=kLoop, calls=%fused_computation.39 | loop fusion | flops 2359296 | bytes 2490404 | tf_op jit(solution)/shard_map/jit(_where)/select_n | solution.py:45
  153.6 0.9 pad_maximum_fusion.2
  155.4 0.9 pad_maximum_fusion.1
  156.2 0.8 convolution_convert_fusion.3
  157.2 0.5 fusion.68
  157.8 0.8 convolution_convert_fusion.2
  158.8 0.5 fusion.67
  159.3 0.8 convolution_convert_fusion.1
  160.3 0.5 fusion.66
  160.9 0.8 convolution_convert_fusion
  161.9 1.0 pad_maximum_fusion
  (41 shorter events, 1.8 us)
Async XLA Ops:
  6.5 138.5 %all-gather.10.cloned.1.call-start = ((), (), s32[]{:S(2)}) async-start(), calls=%async_computation | async-start | bytes 1179648 | tf_op jit(solution)/shard_map/all_gather | solution.py:28
  59.4 16.2 %copy-start = (bf16[128,512]{1,0:T(8,128)(2,1)S(1)}, bf16[128,512]{1,0:T(8,128)(2,1)}, u32[]{:S(2)}) copy-start(bf16[128,512]{1,0:T(8,128)(2,1)} %param.4) | copy-start | bytes 393220
  75.5 75.1 %all-gather.12.cloned.1.call-start = ((), (), s32[]{:S(2)}) async-start(), calls=%async_computation.1 | async-start | bytes 1179648 | tf_op jit(solution)/shard_map/all_gather | solution.py:28
  91.0 14.8 %copy-start.1 = (bf16[128,512]{1,0:T(8,128)(2,1)S(1)}, bf16[128,512]{1,0:T(8,128)(2,1)}, u32[]{:S(2)}) copy-start(bf16[128,512]{1,0:T(8,128)(2,1)} %param.5) | copy-start | bytes 393220
  91.0 16.1 %copy-start.7 = (u32[256]{0:T(256)S(1)}, u32[256]{0:T(256)}, u32[]{:S(2)}) copy-start(u32[256]{0:T(256)} %constant.95) | copy-start | bytes 3076
  106.5 48.6 %collective-permute-start = (bf16[64,512]{1,0:T(8,128)(2,1)}, bf16[64,512]{1,0:T(8,128)(2,1)}, u32[]{:S(2)}, u32[]{:S(2)}) collective-permute-start(bf16[64,512]{1,0:T(8,128)(2,1)} %slice.240), channel_id=1, source_target_pairs={{0,1},{1,2},{2,3},{3,4},{4,5},{5,6},{6,7},{7,8},{8,9},{9,10},{10,1... | collective-permute-start | bytes 196616 | tf_op jit(solution)/shard_map/ppermute | solution.py:40
  109.2 44.4 %collective-permute-start.1 = (bf16[64,512]{1,0:T(8,128)(2,1)}, bf16[64,512]{1,0:T(8,128)(2,1)}, u32[]{:S(2)}, u32[]{:S(2)}) collective-permute-start(bf16[64,512]{1,0:T(8,128)(2,1)} %slice.260), channel_id=1, source_target_pairs={{0,1},{1,2},{2,3},{3,4},{4,5},{5,6},{6,7},{7,8},{8,9},{9,10},{10,1... | collective-permute-start | bytes 196616 | tf_op jit(solution)/shard_map/ppermute | solution.py:40
  147.9 6.5 %copy-start.6 = (bf16[128,1024]{0,1:T(8,128)(2,1)S(1)}, bf16[128,1024]{0,1:T(8,128)(2,1)}, u32[]{:S(2)}) copy-start(bf16[128,1024]{0,1:T(8,128)(2,1)} %copy.36) | copy-start | bytes 786436
  154.5 0.9 copy-start.2
  156.2 1.0 copy-start.5
  157.8 1.0 copy-start.4
  159.3 1.0 copy-start.3
Sparse Core Ops, SparseCore 0:
  75.7 36.2 all-gather.9
  113.8 36.8 all-gather.11
where the time goes:
time: 172 us; the launch traced here: 170 us
  blocking collectives  96.4 us (56%)
  between operations  29.3 us (17%)
  local copies, waits for them, and re-layouts  18.7 us (11%)
  other arithmetic  17.1 us (10%)
  matrix products  5.48 us (3%)
  waiting for transfers between devices  2.74 us (2%)
    all_gather x6, blocking collectives, carried_in(): pieces = jax.tree.map(lambda part: lax.all_gather(part, axis), subtotal)  56.7 us
    unnamed x4, blocking collectives  39.7 us
    unnamed x32, local copies, waits for them, and re-layouts  14.1 us
    select_n x11, other arithmetic, first_seen(): jnp.where(chosen, mine, theirs)  12.9 us
  transfers between devices with their start and end apart: 4, of which 1 were waited for; matrix products, arithmetic and copies ran while one was open for 12% of the time, Pallas kernels for 0%

commit v1 on v0

v1 whole, which is shorter than its diff:
```python
import functools
import math

import jax
import jax.numpy as jnp
from jax import lax
from jax.experimental import pallas as pl
from jax.experimental.pallas import tpu as pltpu
from jax.sharding import PartitionSpec as P

HEADS = 32
KV = 4
D = 128
T = 128
HALO = 64
Z, X, Y = 8, 4, 4
NDEV = 256
PIECES = 2 * KV
SCALE = 1.0 / math.sqrt(D)
NEG = -1e30
UNITS = 16
SIZES = {"z": Z, "x": X, "y": Y}
ORDERS = ("zxy", "xyz", "yxz")
PIECE_ORDER = (0, 1, 2, 1, 0, 2, 1, 2)
FAR_FIRST = {8: (4, 3, 5, 2, 6, 1, 7), 4: (2, 1, 3)}
MESH = pl.DeviceIdType.MESH


def device(c, core):
    return ((c["z"] * X + c["x"]) * Y + c["y"]) * 2 + core


def where(flag, a, b):
    return jnp.where(flag, jnp.int32(a), jnp.int32(b))


def kernel(q_ref, k_ref, v_ref, o_ref, q, kl, vl, anc, m1, acc, pa, local_sem, q_sem, anchor_sem, halo_sem, halo_send, send_sem):
    me = lax.axis_index("seq")
    core = me % 2
    c = {"y": (me // 2) % Y, "x": (me // (2 * Y)) % X, "z": me // (2 * Y * X)}
    sibling = me + 1 - 2 * core
    at0 = {a: c[a] == 0 for a in "zxy"}
    root_chip = at0["z"] & at0["x"] & at0["y"]
    root = me == 0
    relay = jnp.where(root_chip, core == 0, core == 1)
    barrier = pltpu.get_barrier_semaphore()

    def greet(target):
        pl.semaphore_signal(barrier, inc=1, device_id=(target,), device_id_type=MESH)

    @pl.when(jnp.logical_not(relay))
    def _():
        greet(sibling)

    @pl.when(me > 0)
    def _():
        greet(me - 1)

    expected = where(me < NDEV - 1, 1, 0) + where(relay, 1, 0)
    for order in ORDERS:
        a, b, d = order
        parent = dict(c)
        last = jnp.logical_not(at0[d])
        mid = jnp.logical_not(at0[b])
        parent[d] = jnp.int32(0)
        parent[b] = where(last, c[b], 0)
        parent[a] = where(last | mid, c[a], 0)
        to_root = at0["z"] if False else (parent["z"] + parent["x"] + parent["y"]) == 0
        owner = device(parent, where(to_root, 0, 1))

        @pl.when(relay & jnp.logical_not(root))
        def _():
            greet(owner)

        expected = expected + where(relay & at0[d], SIZES[d] - 1, 0)
        expected = expected + where(relay & at0[d] & at0[b], SIZES[b] - 1, 0)
        expected = expected + where(root, SIZES[a] - 1, 0)

    locals_ = []
    for h in range(KV):
        cols = pl.ds(h * D, D)
        locals_.append(pltpu.make_async_copy(k_ref.at[:, cols], kl.at[h, pl.ds(HALO, T), :], local_sem.at[h]))
        locals_.append(pltpu.make_async_copy(v_ref.at[:, cols], vl.at[h, pl.ds(HALO, T), pl.ds(0, D)], local_sem.at[KV + h]))
    roots = []
    for p in range(PIECES):
        src = (k_ref if p < KV else v_ref).at[:, pl.ds((p % KV) * D, D)]
        roots.append(pltpu.make_async_copy(src, anc.at[p], anchor_sem.at[p]))

    @pl.when(root)
    def _():
        for copy in roots:
            copy.start()

    for copy in locals_:
        copy.start()
    for g in range(HEADS):
        pltpu.make_async_copy(q_ref.at[:, pl.ds(g * D, D)], q.at[g // 2, pl.ds((g % 2) * T, T), :], q_sem).start()
    for h in range(KV):
        vl[h, :, D:] = jnp.ones((HALO + T, D), jnp.bfloat16)

    @pl.when(root)
    def _():
        for h in range(KV):
            kl[h, :HALO, :] = jnp.zeros((HALO, D), jnp.bfloat16)
            vl[h, :HALO, :D] = jnp.zeros((HALO, D), jnp.bfloat16)

    pl.semaphore_wait(barrier, expected)

    halos = []
    for h in range(KV):
        rows, cols = pl.ds(T - HALO, HALO), pl.ds(h * D, D)
        for i, (src, dst) in enumerate(((k_ref, kl), (v_ref, vl))):
            halos.append(
                pltpu.make_async_remote_copy(
                    src_ref=src.at[rows, cols],
                    dst_ref=dst.at[h, pl.ds(0, HALO), pl.ds(0, D)],
                    send_sem=halo_send.at[2 * h + i],
                    recv_sem=halo_sem.at[2 * h + i],
                    device_id=(me + 1,),
                    device_id_type=MESH,
                )
            )

    def sends(p):
        a, b, d = ORDERS[PIECE_ORDER[p]]
        out = []
        slot = 0
        for axis, flag in ((a, root), (b, relay & at0[b] & at0[d]), (d, relay & at0[d])):
            for off in FAR_FIRST[SIZES[axis]]:
                to = dict(c)
                to[axis] = (c[axis] + off) % SIZES[axis]
                out.append((flag, slot, device(to, 1)))
                slot += 1
        out.append((relay, slot, sibling))
        return out

    def remote(p, slot, target):
        return pltpu.make_async_remote_copy(
            src_ref=anc.at[p],
            dst_ref=anc.at[p],
            send_sem=send_sem.at[p, slot],
            recv_sem=anchor_sem.at[p],
            device_id=(target,),
            device_id_type=MESH,
        )

    def forward(p):
        pltpu.make_async_copy(anc.at[p], anc.at[p], anchor_sem.at[p]).wait()
        for flag, slot, target in sends(p):
            @pl.when(flag)
            def _():
                remote(p, slot, target).start()

    @pl.when(root)
    def _():
        for p in range(PIECES):
            forward(p)

    @pl.when(me < NDEV - 1)
    def _():
        for copy in halos:
            copy.start()

    for copy in locals_:
        copy.wait()
    pltpu.make_async_copy(q, q, q_sem).wait()

    @pl.when(me > 0)
    def _():
        for copy in halos:
            copy.wait_recv()

    columns = lax.broadcasted_iota(jnp.int32, (2 * T, HALO + T), 1)
    rows = lax.broadcasted_iota(jnp.int32, (2 * T, HALO + T), 0) % T
    seen = (columns - HALO) <= rows
    seen = seen & ((columns >= HALO) | (me > 0))

    def near(u, _):
        h = u // (UNITS // KV)
        s = lax.dot_general(q[u], kl[h], (((1,), (1,)), ((), ())), preferred_element_type=jnp.float32) * SCALE
        s = jnp.where(seen, s, NEG)
        top = jnp.max(s, axis=-1, keepdims=True)
        p = jnp.exp(s - top).astype(jnp.bfloat16)
        m1[u] = jnp.broadcast_to(top, (2 * T, D))
        acc[u] = jnp.dot(p, vl[h], preferred_element_type=jnp.float32)
        return 0

    lax.fori_loop(0, UNITS, near, 0)

    @pl.when(jnp.logical_not(root))
    def _():
        for p in range(PIECES):
            forward(p)

    def far_keys(u, _):
        h = u // (UNITS // KV)
        s = lax.dot_general(q[u], anc[h], (((1,), (1,)), ((), ())), preferred_element_type=jnp.float32) * SCALE
        s = jnp.where(me > 0, s, NEG)
        old = m1[u]
        top = jnp.maximum(jnp.max(s, axis=-1, keepdims=True), old)
        pa[u] = jnp.exp(s - top).astype(jnp.bfloat16)
        fade = jnp.exp(old - top)
        acc[u] = acc[u] * jnp.concatenate([fade, fade], axis=1)
        return 0

    lax.fori_loop(0, UNITS, far_keys, 0)

    def far_values(u, _):
        h = u // (UNITS // KV)
        v = jnp.concatenate([anc[KV + h], jnp.ones((T, D), jnp.bfloat16)], axis=1)
        total = acc[u] + jnp.dot(pa[u], v, preferred_element_type=jnp.float32)
        out = (total[:, :D] / total[:, D:]).astype(jnp.bfloat16)
        o_ref[:, pl.ds(pl.multiple_of(u * 2 * D, D), D)] = out[:T]
        o_ref[:, pl.ds(pl.multiple_of(u * 2 * D + D, D), D)] = out[T:]
        return 0

    lax.fori_loop(0, UNITS, far_values, 0)

    @pl.when(me < NDEV - 1)
    def _():
        for copy in halos:
            copy.wait_send()

    for p in range(PIECES):
        for flag, slot, target in sends(p):
            @pl.when(flag)
            def _():
                remote(p, slot, target).wait_send()


def shards(queries, keys, values):
    return pl.pallas_call(
        kernel,
        out_shape=jax.ShapeDtypeStruct((T, HEADS * D), jnp.bfloat16),
        in_specs=[pl.BlockSpec(memory_space=pl.ANY)] * 3,
        out_specs=pl.BlockSpec(memory_space=pltpu.VMEM),
        scratch_shapes=[
            pltpu.VMEM((UNITS, 2 * T, D), jnp.bfloat16),
            pltpu.VMEM((KV, HALO + T, D), jnp.bfloat16),
            pltpu.VMEM((KV, HALO + T, 2 * D), jnp.bfloat16),
            pltpu.VMEM((PIECES, T, D), jnp.bfloat16),
            pltpu.VMEM((UNITS, 2 * T, D), jnp.float32),
            pltpu.VMEM((UNITS, 2 * T, 2 * D), jnp.float32),
            pltpu.VMEM((UNITS, 2 * T, D), jnp.bfloat16),
            pltpu.SemaphoreType.DMA((2 * KV,)),
            pltpu.SemaphoreType.DMA,
            pltpu.SemaphoreType.DMA((PIECES,)),
            pltpu.SemaphoreType.DMA((2 * KV,)),
            pltpu.SemaphoreType.DMA((2 * KV,)),
            pltpu.SemaphoreType.DMA((PIECES, 14)),
        ],
        compiler_params=pltpu.CompilerParams(collective_id=0, has_side_effects=True),
    )(queries, keys, values)


def solution(mesh):
    return jax.shard_map(
        shards,
        mesh=mesh,
        in_specs=(P("seq", None),) * 3,
        out_specs=P("seq", None),
        check_vma=False,
    )
```

time: 172 us -> 38.9 us (0.23)
  the two profiles are of different devices: /device:TPU:96 before, /device:TPU:44 now
where the time goes in v1:
time: 38.9 us; the launch traced here: 38.6 us
  Pallas kernels  36.4 us (94%)
  local copies, waits for them, and re-layouts  2.29 us (6%)
    pallas_call x1, Pallas kernels, shards(): pl.pallas_call(kernel, out_shape=jax.ShapeDtypeStruct((T, HEADS * D), jnp...  36.4 us
    unnamed x1, local copies, waits for them, and re-layouts  2.29 us

profile of v1, /device:TPU:44, one launch (start us, length us, event | category | flops | bytes accessed | tf_op | source)
XLA Modules:
  0.0 38.6 jit_solution(3788141981084334204)
XLA Ops:
  0.0 36.4 %shard_map.37 = bf16[128,4096]{1,0:T(8,128)(2,1)} custom-call(bf16[128,4096]{1,0:T(8,128)(2,1)} %q_ref.1, bf16[128,512]{1,0:T(8,128)(2,1)} %k_ref.1, bf16[128,512]{1,0:T(8,128)(2,1)} %v_ref.1), custom_call_target="tpu_custom_call" | custom-call | tf_op jit(solution)/shard_map/pallas_call | solution.py:232
  36.4 2.3 %copy.5 = bf16[128,4096]{1,0:T(8,128)(2,1)} copy(bf16[128,4096]{1,0:T(8,128)(2,1)} %shard_map.37) | data formatting | bytes 2097152
